TPU v7x, 32 devices: a whole 2x2x4 slice. The times are simulated.
32 devices in a mesh: pb: 4 (over y, core), pa: 8 (over z, x).
Axes of the slice: x: 2, y: 2, z: 4, core: 2. Of those that a mesh axis runs over, the one named last changes fastest.
Arguments:
- query_hidden: bfloat16 [32, 32, 2048], P('pb', 'pa'), may hold values from -32 to 32
- page_hidden: bfloat16 [8, 1024, 2048], P('pa', 'pb'), may hold values from -4.2 to 4.2
- projection: bfloat16 [2048, 128], replicated, may hold values from -0.125 to 0.125
- clicks: int32 [32, 8, 2], P('pb'), may hold values from 0 to 7, as said below
- bins: int32 [32, 8], P('pb'), may hold values from 0 to 7
Outputs:
- query_grad: bfloat16 [32, 32, 2048], P('pb', 'pa')
- page_grad: bfloat16 [8, 1024, 2048], P('pa', 'pb')
- weight_grad: float32 [2048, 128], P(('pb', 'pa'))
Inputs may be any that keep to these rules, and one draw needn't show every extreme that they name: `clicks`: the two pages of a pair always differ.
All inputs are finite; a program needn't handle non-finite values.
Results may differ from a plain program's by a relative error of at most 0.019.
Values may be sent and summed in bfloat16 or wider, within the bound.
A program may use at most 64 MiB of HBM per device.

v0:
```python
import jax
import jax.numpy as jnp
from jax import lax
from jax.sharding import PartitionSpec as P

sharpness = 0.25


def from_behind(value, axis, steps):
    count = lax.axis_size(axis)
    pairs = [(source, (source + steps) % count) for source in range(count)]
    return lax.ppermute(value, axis, pairs)


def logits(token_rows, patch_rows):
    return sharpness * lax.dot_general(
        token_rows, patch_rows, (((1,), (1,)), ((), ())), preferred_element_type=jnp.float32
    )


def shards(query_hidden, page_hidden, projection, clicks, bins):
    query_count, token_local, hidden_width = query_hidden.shape
    page_count, patch_local, _ = page_hidden.shape
    embed_width = projection.shape[1]
    own_embed = jnp.dot(
        query_hidden.reshape(-1, hidden_width), projection, preferred_element_type=jnp.float32
    ).astype(jnp.bfloat16)
    own_embed = own_embed.reshape(query_count, token_local, embed_width)
    tok_rows = lax.all_gather(own_embed, "pa", axis=1, tiled=True).reshape(-1, embed_width)
    row_count = tok_rows.shape[0]
    query_tokens = row_count // query_count
    page_embed = jnp.dot(
        page_hidden.reshape(-1, hidden_width), projection, preferred_element_type=jnp.float32
    ).astype(jnp.bfloat16)
    page_embed = page_embed.reshape(page_count, patch_local, embed_width)
    start_state = (
        jnp.full((row_count, page_count), -1e30, jnp.float32),
        jnp.zeros((row_count, page_count), jnp.float32),
    )
    run_max, run_sum = start_state
    logit_block = logits(tok_rows, lax.all_gather(page_embed, "pb", axis=1, tiled=True)[0])
    new_max = jnp.maximum(run_max[:, 0], jnp.max(logit_block, axis=1))
    new_sum = run_sum[:, 0] * jnp.exp(run_max[:, 0] - new_max)
    new_sum = new_sum + jnp.sum(jnp.exp(logit_block - new_max[:, None]), axis=1)
    max_list = [new_max]
    sum_list = [new_sum]
    run_max = jnp.stack(max_list, axis=1)
    run_sum = jnp.stack(sum_list, axis=1)
    log_norm = run_max + jnp.log(run_sum)
    query_score = log_norm.reshape(query_count, query_tokens, page_count).sum(axis=1)
    owned_pages = lax.axis_index("pa") * page_count + jnp.arange(page_count, dtype=jnp.int32)
    positive = clicks[:, :, 0]
    negative = clicks[:, :, 1]
    hit_pos = (positive[:, :, None] == owned_pages).astype(jnp.float32)
    hit_neg = (negative[:, :, None] == owned_pages).astype(jnp.float32)
    score_table = lax.all_gather(query_score, "pa", axis=1, tiled=True)
    page_ids = jnp.arange(score_table.shape[1], dtype=jnp.int32)
    table_pos = (positive[:, :, None] == page_ids).astype(jnp.float32)
    table_neg = (negative[:, :, None] == page_ids).astype(jnp.float32)
    pair_gap = jnp.sum(table_pos * score_table[:, None, :], axis=2) - jnp.sum(
        table_neg * score_table[:, None, :], axis=2
    )
    pair_weight = jnp.sqrt(bins.astype(jnp.float32) + 1.0)
    pair_coeff = -pair_weight * jax.nn.sigmoid(-pair_gap)
    score_grad = jnp.sum(pair_coeff[:, :, None] * (hit_pos - hit_neg), axis=1)
    grad_rows = jnp.repeat(score_grad, query_tokens, axis=0)
    norm_cols = jnp.repeat(log_norm, patch_local, axis=1)
    grad_cols = jnp.repeat(grad_rows, patch_local, axis=1)

    def cycle_turn(turn_index, cycle_state):
        patch_block, patch_accum, token_acc = cycle_state
        block_rows = patch_block.reshape(-1, embed_width)
        logit_block = logits(tok_rows, block_rows)
        soft_grad = (grad_cols * jnp.exp(logit_block - norm_cols)).astype(jnp.bfloat16)
        token_acc = token_acc + jnp.dot(soft_grad, block_rows, preferred_element_type=jnp.float32)
        patch_part = lax.dot_general(
            soft_grad, tok_rows, (((0,), (0,)), ((), ())), preferred_element_type=jnp.float32
        )
        patch_accum = patch_accum + patch_part.reshape(patch_accum.shape)
        patch_block = from_behind(patch_block, "pb", 1)
        patch_accum = from_behind(patch_accum.astype(jnp.bfloat16), "pb", 1).astype(
            patch_accum.dtype
        )
        return (patch_block, patch_accum, token_acc)

    start_state = (
        page_embed,
        jnp.zeros(page_embed.shape, jnp.float32),
        jnp.zeros((row_count, embed_width), jnp.float32),
    )
    _, patch_acc, token_acc = lax.fori_loop(0, lax.axis_size("pb"), cycle_turn, start_state)
    token_own = lax.psum_scatter(
        token_acc.reshape(query_count, query_tokens, embed_width).astype(jnp.bfloat16),
        "pa",
        scatter_dimension=1,
        tiled=True,
    ).astype(jnp.float32)
    token_low = (sharpness * token_own).astype(jnp.bfloat16).reshape(-1, embed_width)
    patch_low = (sharpness * patch_acc).astype(jnp.bfloat16).reshape(-1, embed_width)
    query_grad = lax.dot_general(
        token_low, projection, (((1,), (1,)), ((), ())), preferred_element_type=jnp.float32
    )
    query_grad = query_grad.astype(jnp.bfloat16).reshape(query_hidden.shape)
    page_grad = lax.dot_general(
        patch_low, projection, (((1,), (1,)), ((), ())), preferred_element_type=jnp.float32
    )
    page_grad = page_grad.astype(jnp.bfloat16).reshape(page_hidden.shape)
    weight_term = lax.dot_general(
        query_hidden.reshape(-1, hidden_width),
        token_low,
        (((0,), (0,)), ((), ())),
        preferred_element_type=jnp.float32,
    )
    weight_term = weight_term + lax.dot_general(
        page_hidden.reshape(-1, hidden_width),
        patch_low,
        (((0,), (0,)), ((), ())),
        preferred_element_type=jnp.float32,
    )
    weight_grad = lax.psum_scatter(weight_term, ("pb", "pa"), scatter_dimension=0, tiled=True)
    return (query_grad, page_grad, weight_grad)


def solution(mesh):
    return jax.shard_map(
        shards,
        mesh=mesh,
        in_specs=(
            P("pb", "pa", None),
            P("pa", "pb", None),
            P(),
            P("pb", None, None),
            P("pb", None),
        ),
        out_specs=(P("pb", "pa", None), P("pa", "pb", None), P(("pb", "pa"), None)),
        check_vma=False,
    )
```

profile of v0, /device:TPU:0, one launch (start us, length us, event | category | flops | bytes accessed | tf_op | source)
XLA Modules:
  0.0 294.6 jit_solution(1814558097921956855)
XLA Ops:
  7.2 1.2 copy-done
  8.4 1.5 convolution_convert_fusion.2
  9.9 7.3 %all-gather = bf16[1024,128]{1,0:T(8,128)(2,1)S(1)} all-gather(bf16[256,128]{1,0:T(8,128)(2,1)S(1)} %convolution_convert_fusion.2), channel_id=2, replica_groups=mesh['pb'=4,'pa'=8] {'pb'}, dimensions={0}, use_global_device_ids=true | all-gather | bytes 327680 | tf_op jit(solution)/shard_map/all_gather | solution.py:41
  17.2 0.2 convolution_convert_fusion.3
  17.5 30.9 %all_gather.9 = bf16[8,32,128]{2,0,1:T(8,128)(2,1)S(1)} all-gather(bf16[8,4,128]{2,0,1:T(8,128)(2,1)S(1)} %copy.36), channel_id=1, replica_groups=mesh['pb'=4,'pa'=8] {'pa'}, dimensions={1}, use_global_device_ids=true | all-gather | bytes 73728 | tf_op jit(solution)/shard_map/all_gather | solution.py:29
  48.4 0.4 fusion.24
  48.8 0.1 max_squeeze.20
  48.8 0.3 exponential_reduce_fusion
  49.1 0.1 reduce_sum.50
  49.3 0.1 add_reduce_fusion
  49.4 20.5 %all-gather.1 = f32[8,1,8]{2,1,0:T(1,128)S(1)} all-gather(f32[1,1,8]{2,1,0:T(1,128)S(1)} %bitcast.83), channel_id=1, replica_groups=mesh['pb'=4,'pa'=8] {'pa'}, dimensions={0}, use_global_device_ids=true | all-gather | bytes 288 | tf_op jit(solution)/shard_map/all_gather | solution.py:56
  69.8 0.1 copy.39
  69.9 0.2 select_reduce_fusion
  70.1 0.1 fusion.20
  70.2 0.1 broadcast_in_dim.24
  70.3 0.1 broadcast_in_dim.25
  70.4 18.0 %while.15 = (s32[]{:T(128)}, bf16[1,256,128]{2,1,0:T(8,128)(2,1)S(1)}, f32[1,256,128]{2,1,0:T(8,128)S(1)}, f32[256,128]{1,0:T(8,128)S(1)}, bf16[256,128]{1,0:T(8...) while((s32[]{:T(128)}, bf16[1,256,128]{2,1,0:T(8,128)(2,1)S(1)}, ...), condition=%wide.region_7.0_spmd.clone, body=%wide.region_6.0_spmd.clone.sunk | while | flops 50790400 | bytes 1968312 | solution.py:91
  70.4 0.1 collective-permute-start
  70.5 0.2 fusion.51
  70.7 0.2 fusion.52
  70.9 1.7 collective-permute-start.1
  72.6 0.2 convolution_add_fusion.3
  72.8 2.1 collective-permute-done.1
  74.9 0.1 collective-permute-start
  75.0 0.2 fusion.51
  75.2 0.2 fusion.52
  75.4 1.7 collective-permute-start.1
  77.1 0.2 convolution_add_fusion.3
  77.3 2.1 collective-permute-done.1
  79.5 0.2 fusion.51
  79.7 0.2 fusion.52
  79.9 1.7 collective-permute-start.1
  81.6 0.2 convolution_add_fusion.3
  81.8 2.1 collective-permute-done.1
  84.0 0.2 fusion.51
  84.2 0.2 fusion.52
  84.4 1.7 collective-permute-start.1
  86.1 0.2 convolution_add_fusion.3
  86.3 2.1 collective-permute-done.1
  88.4 0.7 copy.41
  89.1 59.9 %reduce-scatter.5.cloned.1.call-done = bf16[8,4,128]{2,0,1:T(8,128)(2,1)} async-done(((bf16[8,32,128]{2,0,1:T(8,128)(2,1)}), bf16[8,4,128]{2,0,1:T(8,128)(2,1)}) %reduce-scatter.5.cloned.1.call-update) | async-done | bytes 8208 | tf_op jit(solution)/shard_map/reduce_scatter | solution.py:92
  149.0 1.0 convolution_bitcast_fusion.1
  150.0 0.3 fusion.13
  150.4 1.3 copy.45
  151.8 1.4 fusion.12
  153.2 0.3 convolution_convert_fusion.1
  153.5 0.7 reshape.115
  154.2 133.5 %reduce-scatter.7.cloned.1.call-done = f32[64,128]{1,0:T(8,128)} async-done(((f32[2048,128]{1,0:T(8,128)}), f32[64,128]{1,0:T(8,128)}) %reduce-scatter.7.cloned.1.call-update) | async-done | bytes 32784
  (40 shorter events, 0.4 us)
Async XLA Ops:
  7.2 1.2 copy-start
  7.2 10.0 %copy-start.2 = (bf16[8,4,2048]{2,1,0:T(4,128)(2,1)S(1)}, bf16[8,4,2048]{2,1,0:T(4,128)(2,1)}, u32[]{:S(2)}) copy-start(bf16[8,4,2048]{2,1,0:T(4,128)(2,1)} %param.7) | copy-start | bytes 393220
  7.2 141.8 %reduce-scatter.5.cloned.1.call-start = ((), (), s32[]{:S(2)}) async-start(), calls=%async_computation.2 | async-start | bytes 73728 | tf_op jit(solution)/shard_map/reduce_scatter | solution.py:92
  8.4 8.8 %copy-start.1 = (bf16[2048,128]{1,0:T(8,128)(2,1)S(1)}, bf16[2048,128]{1,0:T(8,128)(2,1)}, u32[]{:S(2)}) copy-start(bf16[2048,128]{1,0:T(8,128)(2,1)} %param.9) | copy-start | bytes 1572868
  48.3 21.6 %copy-start.4 = (s32[8,8,2]{1,2,0:T(2,128)S(1)}, s32[8,8,2]{1,2,0:T(2,128)}, u32[]{:S(2)}) copy-start(s32[8,8,2]{1,2,0:T(2,128)} %param.10) | copy-start | bytes 1540
  48.4 21.7 %copy-start.5 = (s32[8,8]{1,0:T(8,128)S(1)}, s32[8,8]{1,0:T(8,128)}, u32[]{:S(2)}) copy-start(s32[8,8]{1,0:T(8,128)} %param.11) | copy-start | bytes 772
  70.4 4.5 %collective-permute-start = (bf16[1,256,128]{2,1,0:T(8,128)(2,1)S(1)}, bf16[1,256,128]{2,1,0:T(8,128)(2,1)S(1)}, u32[]{:S(2)}, u32[]{:S(2)}) collective-permute-start(bf16[1,256,128]{2,1,0:T(8,128)(2,1)S(1)} %copy.56), channel_id=1, source_target_pairs={{0,8},{8,16},{16,24},{24,0},{1,9},{9,17},{17,25},{25,1},{2,10},{10... | collective-permute-start | bytes 196616 | tf_op jit(solution)/shard_map/while/body/eval_jaxpr/ppermute | solution.py:12
  70.9 3.9 %collective-permute-start.1 = (bf16[1,256,128]{2,1,0:T(8,128)(2,1)S(1)}, bf16[1,256,128]{2,1,0:T(8,128)(2,1)S(1)}, u32[]{:S(2)}, u32[]{:S(2)}) collective-permute-start(bf16[1,256,128]{2,1,0:T(8,128)(2,1)S(1)} %fusion.52), channel_id=1, source_target_pairs={{0,8},{8,16},{16,24},{24,0},{1,9},{9,17},{17,25},{25,1},{2,10},{10... | collective-permute-start | bytes 196616 | tf_op jit(solution)/shard_map/while/body/eval_jaxpr/ppermute | solution.py:12
  74.9 4.5 %collective-permute-start = (bf16[1,256,128]{2,1,0:T(8,128)(2,1)S(1)}, bf16[1,256,128]{2,1,0:T(8,128)(2,1)S(1)}, u32[]{:S(2)}, u32[]{:S(2)}) collective-permute-start(bf16[1,256,128]{2,1,0:T(8,128)(2,1)S(1)} %copy.56), channel_id=1, source_target_pairs={{0,8},{8,16},{16,24},{24,0},{1,9},{9,17},{17,25},{25,1},{2,10},{10... | collective-permute-start | bytes 196616 | tf_op jit(solution)/shard_map/while/body/eval_jaxpr/ppermute | solution.py:12
  75.4 3.9 %collective-permute-start.1 = (bf16[1,256,128]{2,1,0:T(8,128)(2,1)S(1)}, bf16[1,256,128]{2,1,0:T(8,128)(2,1)S(1)}, u32[]{:S(2)}, u32[]{:S(2)}) collective-permute-start(bf16[1,256,128]{2,1,0:T(8,128)(2,1)S(1)} %fusion.52), channel_id=1, source_target_pairs={{0,8},{8,16},{16,24},{24,0},{1,9},{9,17},{17,25},{25,1},{2,10},{10... | collective-permute-start | bytes 196616 | tf_op jit(solution)/shard_map/while/body/eval_jaxpr/ppermute | solution.py:12
  79.4 4.5 %collective-permute-start = (bf16[1,256,128]{2,1,0:T(8,128)(2,1)S(1)}, bf16[1,256,128]{2,1,0:T(8,128)(2,1)S(1)}, u32[]{:S(2)}, u32[]{:S(2)}) collective-permute-start(bf16[1,256,128]{2,1,0:T(8,128)(2,1)S(1)} %copy.56), channel_id=1, source_target_pairs={{0,8},{8,16},{16,24},{24,0},{1,9},{9,17},{17,25},{25,1},{2,10},{10... | collective-permute-start | bytes 196616 | tf_op jit(solution)/shard_map/while/body/eval_jaxpr/ppermute | solution.py:12
  79.9 3.9 %collective-permute-start.1 = (bf16[1,256,128]{2,1,0:T(8,128)(2,1)S(1)}, bf16[1,256,128]{2,1,0:T(8,128)(2,1)S(1)}, u32[]{:S(2)}, u32[]{:S(2)}) collective-permute-start(bf16[1,256,128]{2,1,0:T(8,128)(2,1)S(1)} %fusion.52), channel_id=1, source_target_pairs={{0,8},{8,16},{16,24},{24,0},{1,9},{9,17},{17,25},{25,1},{2,10},{10... | collective-permute-start | bytes 196616 | tf_op jit(solution)/shard_map/while/body/eval_jaxpr/ppermute | solution.py:12
  83.9 4.5 %collective-permute-start = (bf16[1,256,128]{2,1,0:T(8,128)(2,1)S(1)}, bf16[1,256,128]{2,1,0:T(8,128)(2,1)S(1)}, u32[]{:S(2)}, u32[]{:S(2)}) collective-permute-start(bf16[1,256,128]{2,1,0:T(8,128)(2,1)S(1)} %copy.56), channel_id=1, source_target_pairs={{0,8},{8,16},{16,24},{24,0},{1,9},{9,17},{17,25},{25,1},{2,10},{10... | collective-permute-start | bytes 196616 | tf_op jit(solution)/shard_map/while/body/eval_jaxpr/ppermute | solution.py:12
  84.4 3.9 %collective-permute-start.1 = (bf16[1,256,128]{2,1,0:T(8,128)(2,1)S(1)}, bf16[1,256,128]{2,1,0:T(8,128)(2,1)S(1)}, u32[]{:S(2)}, u32[]{:S(2)}) collective-permute-start(bf16[1,256,128]{2,1,0:T(8,128)(2,1)S(1)} %fusion.52), channel_id=1, source_target_pairs={{0,8},{8,16},{16,24},{24,0},{1,9},{9,17},{17,25},{25,1},{2,10},{10... | collective-permute-start | bytes 196616 | tf_op jit(solution)/shard_map/while/body/eval_jaxpr/ppermute | solution.py:12
  89.1 198.6 %reduce-scatter.7.cloned.1.call-start = ((), (), s32[]{:S(2)}) async-start(), calls=%async_computation.3 | async-start | bytes 1081344
  151.7 1.4 copy-start.3
Sparse Core Ops, SparseCore 0:
  89.2 59.7 reduce-scatter.4
  151.9 135.8 reduce-scatter.6
where the time goes:
time: 295 us
  waiting for transfers between devices  202 us (68%)
  blocking collectives  58.6 us (20%)
  between operations  14.2 us (5%)
  matrix products  7.66 us (3%)
  starting transfers between devices  6.98 us (2%)
  local copies, waits for them, and re-layouts  4.37 us (1%)
    unnamed x3, waiting for transfers between devices  134 us
    reduce_scatter x1, waiting for transfers between devices, shards(): lax.psum_scatter(token_acc.reshape(query_count, query_tokens, embed_width...  59.9 us
    all_gather x1, blocking collectives, shards(): lax.all_gather(own_embed, 'pa', axis=1, tiled=True).reshape(-1, embed_width)  30.9 us
    all_gather x1, blocking collectives, shards(): score_table = lax.all_gather(query_score, 'pa', axis=1, tiled=True)  20.5 us
    ppermute x8, waiting for transfers between devices, from_behind(): return lax.ppermute(value, axis, pairs)  8.25 us
    all_gather x1, blocking collectives, shards(): lax.all_gather(page_embed, 'pb', axis=1, tiled=True)[0]  7.25 us
    ppermute x8, starting transfers between devices, from_behind(): return lax.ppermute(value, axis, pairs)  6.9 us
  transfers between devices with their start and end apart: 10, of which 6 were waited for; matrix products, arithmetic and copies ran while one was open for 2% of the time, Pallas kernels for 0%

commit v1 on v0

v1 whole, which is shorter than its diff:
```python
import functools

import jax
import jax.numpy as jnp
from jax import lax
from jax.experimental import pallas as pl
from jax.experimental.pallas import tpu as pltpu
from jax.sharding import PartitionSpec as P

sharpness = 0.25
MESH = pl.DeviceIdType.MESH
BF = jnp.bfloat16
F32 = jnp.float32


def dot(x, y, dims):
    return lax.dot_general(x, y, (dims, ((), ())), preferred_element_type=F32)


def kernel(
    PB, PA, qh_ref, ph_ref, proj_ref, pos_ref, neg_ref, weight_ref, mask_ref,
    tlow_ref, plow_ref, w_ref,
    qe, pe, ebuf, sc, gsend, grecv, tsend, trecv, w1send, w1recv, wown, w2send, w2recv,
    qs, qr, ps, pr, ss, sr, gs, gr, ts, tr, us, ur, vs, vr,
):
    b = lax.axis_index("pb")
    a = lax.axis_index("pa")
    rows = qh_ref.shape[0]
    E = proj_ref.shape[1]
    tokens = PA * rows

    def remote(src, dst, send, recv, to_b, to_a):
        return pltpu.make_async_remote_copy(
            src_ref=src, dst_ref=dst, send_sem=send, recv_sem=recv,
            device_id=(to_b, to_a), device_id_type=MESH,
        )

    barrier = pltpu.get_barrier_semaphore()

    def greet(k, carry):
        other = lax.rem(b * PA + a + k, PB * PA)
        pl.semaphore_signal(
            barrier, inc=1, device_id=(other // PA, lax.rem(other, PA)), device_id_type=MESH
        )
        return carry

    lax.fori_loop(1, PB * PA, greet, 0)

    qe[a] = dot(qh_ref[...], proj_ref[...], ((1,), (0,))).astype(BF)
    pe[b] = dot(ph_ref[...], proj_ref[...], ((1,), (0,))).astype(BF)
    pl.semaphore_wait(barrier, PB * PA - 1)

    copies = []
    page_in = {}
    for o in range(1, PB):
        c = remote(pe.at[b], pe.at[b], ps.at[o - 1], pr.at[o - 1], lax.rem(b + o, PB), a)
        c.start()
        page_in[o] = c
    query_in = []
    for o in range(1, PA):
        c = remote(qe.at[a], qe.at[a], qs.at[o - 1], qr.at[o - 1], b, lax.rem(a + o, PA))
        c.start()
        query_in.append(c)
    for c in query_in:
        c.wait_recv()

    tok = qe[...].reshape(tokens, E)
    maxes, sums = [], []
    for o in range(PB):
        j = lax.rem(b + PB - o, PB)
        if o:
            page_in[o].wait_recv()
        block = sharpness * dot(pe[j], tok, ((1,), (1,)))
        top = jnp.max(block, axis=0, keepdims=True)
        e = jnp.exp(block - top)
        ebuf[o] = e
        maxes.append(top)
        sums.append(jnp.sum(e, axis=0, keepdims=True))
    top = functools.reduce(jnp.maximum, maxes)
    shrink = [jnp.exp(m - top) for m in maxes]
    total = functools.reduce(jnp.add, [s * f for s, f in zip(sums, shrink)])
    log_norm = top + jnp.log(total)
    mask = mask_ref[...]
    score = jnp.sum(mask * log_norm, axis=1, keepdims=True)
    sc[a] = jnp.broadcast_to(score, sc.shape[1:])
    score_in = []
    for o in range(1, PA):
        c = remote(sc.at[a], sc.at[a], ss.at[o - 1], sr.at[o - 1], b, lax.rem(a + o, PA))
        c.start()
        score_in.append(c)
    for c in score_in:
        c.wait_recv()

    pos = pos_ref[...]
    neg = neg_ref[...]
    at_pos = jnp.zeros(pos.shape, F32)
    at_neg = jnp.zeros(pos.shape, F32)
    for p in range(PA):
        at_pos = at_pos + jnp.where(pos == p, sc[p], 0.0)
        at_neg = at_neg + jnp.where(neg == p, sc[p], 0.0)
    coeff = -weight_ref[...] * jax.nn.sigmoid(at_neg - at_pos)
    hits = (pos == a).astype(F32) - (neg == a).astype(F32)
    grad = jnp.sum(coeff * hits, axis=1, keepdims=True)
    grad_row = jnp.sum(mask * grad, axis=0, keepdims=True) / total

    token_acc = None
    patch_in = []
    for o in list(range(1, PB)) + [0]:
        j = lax.rem(b + PB - o, PB)
        soft = (ebuf[o] * (grad_row * shrink[o])).astype(BF)
        patch_part = dot(soft, tok, ((1,), (0,)))
        if o:
            gsend[o - 1] = patch_part.astype(BF)
            c = remote(gsend.at[o - 1], grecv.at[o - 1], gs.at[o - 1], gr.at[o - 1], j, a)
            c.start()
            patch_in.append(c)
        else:
            patch_acc = patch_part
        part = dot(soft, pe[j], ((0,), (0,)))
        token_acc = part if token_acc is None else token_acc + part
    for k in range(PA):
        tsend[k] = token_acc[k * rows:(k + 1) * rows].astype(BF)
    token_in = []
    for o in range(1, PA):
        to = lax.rem(a + o, PA)
        c = remote(tsend.at[to], trecv.at[o - 1], ts.at[o - 1], tr.at[o - 1], b, to)
        c.start()
        token_in.append(c)
    token_own = tsend[a].astype(F32)
    for o, c in enumerate(patch_in):
        c.wait_recv()
        patch_acc = patch_acc + grecv[o].astype(F32)
    patch_low = (sharpness * patch_acc).astype(BF)
    plow_ref[...] = patch_low
    for o, c in enumerate(token_in):
        c.wait_recv()
        token_own = token_own + trecv[o].astype(F32)
    token_low = (sharpness * token_own).astype(BF)
    tlow_ref[...] = token_low

    half = PB // 2
    parity = lax.rem(b, 2)
    partner = b + 1 - 2 * parity
    span = w1send.shape[1]
    chunk = w_ref.shape[0]

    def weight_block(index):
        cols = pl.ds(pl.multiple_of(index * span, 128), span)
        return dot(ph_ref[:, cols], patch_low, ((0,), (0,))) + dot(
            qh_ref[:, cols], token_low, ((0,), (0,))
        )

    pair_in = []
    for m in range(half):
        w1send[m] = weight_block(2 * m + 1 - parity).astype(BF)
        c = remote(w1send.at[m], w1recv.at[m], us.at[m], ur.at[m], partner, a)
        c.start()
        pair_in.append(c)
    for m in range(half):
        wown[m] = weight_block(2 * m + parity)
    for m in range(half):
        pair_in[m].wait_recv()
        both = (wown[m] + w1recv[m].astype(F32)).astype(BF)
        for k in range(PA):
            w2send[m * PA + k] = both[k * chunk:(k + 1) * chunk]
    count = half * PA
    mine = (b // 2) * PA + a
    last_in = []
    for o in range(1, count):
        to = lax.rem(mine + o, count)
        c = remote(
            w2send.at[to], w2recv.at[o - 1], vs.at[o - 1], vr.at[o - 1],
            2 * (to // PA) + parity, lax.rem(to, PA),
        )
        c.start()
        last_in.append(c)
    weight = w2send[mine].astype(F32)
    for o, c in enumerate(last_in):
        c.wait_recv()
        weight = weight + w2recv[o].astype(F32)
    w_ref[...] = weight
    for c in list(page_in.values()) + query_in + score_in + patch_in + token_in + pair_in + last_in:
        c.wait_send()


def shards(PB, PA, query_hidden, page_hidden, projection, clicks, bins):
    queries, token_local, hidden = query_hidden.shape
    page_count, patches, _ = page_hidden.shape
    assert page_count == 1 and PB % 2 == 0
    pairs = clicks.shape[1]
    E = projection.shape[1]
    rows = queries * token_local
    tokens = rows * PA
    chunk = hidden // (PB * PA)
    half = PB // 2
    count = half * PA
    lanes = -(-pairs // 128) * 128
    pad = ((0, 0), (0, lanes - pairs))
    pos = jnp.pad(clicks[:, :, 0], pad, constant_values=-1)
    neg = jnp.pad(clicks[:, :, 1], pad, constant_values=-1)
    weight = jnp.pad(jnp.sqrt(bins.astype(F32) + 1.0), pad)
    mask = (
        (jnp.arange(tokens)[None, :] % rows) // token_local == jnp.arange(queries)[:, None]
    ).astype(F32)
    qh = query_hidden.reshape(rows, hidden)
    ph = page_hidden.reshape(patches, hidden)
    vmem = pl.BlockSpec(memory_space=pltpu.VMEM)
    dma = lambda n: pltpu.SemaphoreType.DMA((n,))
    token_low, patch_low, weight_grad = pl.pallas_call(
        functools.partial(kernel, PB, PA),
        out_shape=(
            jax.ShapeDtypeStruct((rows, E), BF),
            jax.ShapeDtypeStruct((patches, E), BF),
            jax.ShapeDtypeStruct((chunk, E), F32),
        ),
        in_specs=[vmem] * 7,
        out_specs=(vmem,) * 3,
        scratch_shapes=[
            pltpu.VMEM((PA, rows, E), BF),
            pltpu.VMEM((PB, patches, E), BF),
            pltpu.VMEM((PB, patches, tokens), F32),
            pltpu.VMEM((PA, queries, lanes), F32),
            pltpu.VMEM((PB - 1, patches, E), BF),
            pltpu.VMEM((PB - 1, patches, E), BF),
            pltpu.VMEM((PA, rows, E), BF),
            pltpu.VMEM((PA - 1, rows, E), BF),
            pltpu.VMEM((half, PA * chunk, E), BF),
            pltpu.VMEM((half, PA * chunk, E), BF),
            pltpu.VMEM((half, PA * chunk, E), F32),
            pltpu.VMEM((count, chunk, E), BF),
            pltpu.VMEM((count - 1, chunk, E), BF),
            dma(PA - 1), dma(PA - 1), dma(PB - 1), dma(PB - 1), dma(PA - 1), dma(PA - 1),
            dma(PB - 1), dma(PB - 1), dma(PA - 1), dma(PA - 1), dma(half), dma(half),
            dma(count - 1), dma(count - 1),
        ],
        compiler_params=pltpu.CompilerParams(
            collective_id=0, has_side_effects=True, vmem_limit_bytes=48 * 1024 * 1024
        ),
        name="fused",
    )(qh, ph, projection, pos, neg, weight, mask)
    query_grad = dot(token_low, projection, ((1,), (1,))).astype(BF).reshape(query_hidden.shape)
    page_grad = dot(patch_low, projection, ((1,), (1,))).astype(BF).reshape(page_hidden.shape)
    return query_grad, page_grad, weight_grad


def solution(mesh):
    return jax.shard_map(
        functools.partial(shards, mesh.shape["pb"], mesh.shape["pa"]),
        mesh=mesh,
        in_specs=(
            P("pb", "pa", None),
            P("pa", "pb", None),
            P(),
            P("pb", None, None),
            P("pb", None),
        ),
        out_specs=(P("pb", "pa", None), P("pa", "pb", None), P(("pb", "pa"), None)),
        check_vma=False,
    )
```

time: 295 us -> 39.6 us (0.13)
  the two profiles are of different devices: /device:TPU:0 before, /device:TPU:1 now
where the time goes in v1:
time: 39.6 us; the launch traced here: 39.3 us
  Pallas kernels  30.9 us (78%)
  local copies, waits for them, and re-layouts  5.35 us (14%)
  matrix products  1.68 us (4%)
  other arithmetic  0.71 us (2%)
  between operations  0.68 us (2%)
    pallas_call x1, Pallas kernels, shards(): pl.pallas_call(functools.partial(kernel, PB, PA), out_shape=(jax.ShapeDty...  30.9 us
    unnamed x7, local copies, waits for them, and re-layouts  2.88 us
    dot_general x2, matrix products, dot(): return lax.dot_general(x, y, (dims, ((), ())), preferred_element_type=F32)  1.68 us
    reshape x1, local copies, waits for them, and re-layouts, shards(): qh = query_hidden.reshape(rows, hidden)  0.94 us

profile of v1, /device:TPU:1, one launch (start us, length us, event | category | flops | bytes accessed | tf_op | source)
XLA Modules:
  0.0 39.3 jit_solution(12879017968934438034)
XLA Ops:
  0.6 0.7 %add_sqrt_fusion = f32[8,8]{1,0:T(8,128)S(1)} fusion(s32[8,8]{1,0:T(8,128)} %param.9), kind=kLoop, calls=%fused_computation.5 | loop fusion | flops 128 | bytes 512 | tf_op jit(solution)/shard_map/sqrt | solution.py:201
  1.4 0.8 %fusion.2 = (s32[8,8,1]{1,2,0:T(1,128)S(1)}, s32[8,8,1]{1,2,0:T(1,128)S(1)}) fusion(s32[8,8,2]{1,2,0:T(2,128)} %param.8), kind=kLoop, calls=%fused_computation.11 | loop fusion | bytes 1024 | tf_op jit(solution)/shard_map/slice | solution.py:200
  2.2 0.9 %reshape.66.qh_ref = bf16[32,2048]{1,0:T(8,128)(2,1)S(1)} reshape(bf16[8,4,2048]{2,1,0:T(4,128)(2,1)} %param.5) | data formatting | bytes 262144 | tf_op jit(solution)/shard_map/reshape | solution.py:205
  3.1 0.0 copy-start
  3.1 1.0 %copy-done = bf16[2048,128]{1,0:T(8,128)(2,1)S(1)} copy-done((bf16[2048,128]{1,0:T(8,128)(2,1)S(1)}, bf16[2048,128]{1,0:T(8,128)(2,1)}, u32[]{:S(2)}) %copy-start) | copy-done | bytes 524312
  4.2 0.0 copy-start.2
  4.2 1.2 %copy-done.2 = bf16[1,256,2048]{2,1,0:T(8,128)(2,1)S(1)} copy-done((bf16[1,256,2048]{2,1,0:T(8,128)(2,1)S(1)}, bf16[1,256,2048]{2,1,0:T(8,128)(2,1)}, u32[]{:S(2)}) %copy-start.2) | copy-done | bytes 1048600
  5.4 0.0 copy-start.1
  5.4 30.9 %fused.1 = (bf16[32,128]{1,0:T(8,128)(2,1)S(1)}, bf16[256,128]{1,0:T(8,128)(2,1)S(1)}, f32[64,128]{1,0:T(8,128)S(1)}) custom-call(bf16[32,2048]{1,0:T(8,128)(2,1)S(1)} %reshape.66.qh_ref, bf16[256,2048]{1,0:T(8,128)(2,1)S(1)} %bitcast.13, bf16[2048,128]{1,0:T(8,128)(2,1)S(1)} %copy-done, s32[8,128]{1,0:T(8,128)S(1)} %pad.11.pos_ref, ...), custom_call_target="tpu_custom_call" | custom-call | tf_op jit(solution)/shard_map/fused/pallas_call | solution.py:209
  36.3 0.3 convolution_convert_fusion.1
  36.5 0.7 %reshape.68 = bf16[8,4,2048]{2,1,0:T(4,128)(2,1)} reshape(bf16[32,2048]{1,0:T(8,128)(2,1)S(1)} %convolution_convert_fusion.1) | data formatting | bytes 262144 | tf_op jit(solution)/shard_map/reshape | solution.py:241
  37.3 0.0 copy-done.1
  37.3 1.4 %fusion = bf16[1,256,2048]{2,1,0:T(8,128)(2,1)} fusion(bf16[256,128]{1,0:T(8,128)(2,1)S(1)} %get-tuple-element.7, bf16[2048,128]{1,0:T(8,128)(2,1)S(1)} %copy-done.1), kind=kOutput, calls=%fused_computation.1 | convolution fusion | flops 134742016 | bytes 1638400 | tf_op jit(solution)/shard_map/dot_general | solution.py:17
  38.7 0.6 %copy.13 = f32[64,128]{1,0:T(8,128)} copy(f32[64,128]{1,0:T(8,128)S(1)} %get-tuple-element.16) | data formatting | bytes 65536
  (5 shorter events, 0.0 us)
Async XLA Ops:
  3.1 1.0 %copy-start = (bf16[2048,128]{1,0:T(8,128)(2,1)S(1)}, bf16[2048,128]{1,0:T(8,128)(2,1)}, u32[]{:S(2)}) copy-start(bf16[2048,128]{1,0:T(8,128)(2,1)} %proj_ref.1) | copy-start | bytes 1572868
  4.2 1.2 %copy-start.2 = (bf16[1,256,2048]{2,1,0:T(8,128)(2,1)S(1)}, bf16[1,256,2048]{2,1,0:T(8,128)(2,1)}, u32[]{:S(2)}) copy-start(bf16[1,256,2048]{2,1,0:T(8,128)(2,1)} %param.6) | copy-start | bytes 3145732
  5.4 31.9 %copy-start.1 = (bf16[2048,128]{1,0:T(8,128)(2,1)S(1)}, bf16[2048,128]{1,0:T(8,128)(2,1)}, u32[]{:S(2)}) copy-start(bf16[2048,128]{1,0:T(8,128)(2,1)} %proj_ref.1) | copy-start | bytes 1572868

commit v2 on v1

v2 whole, which is shorter than its diff:
```python
import functools

import jax
import jax.numpy as jnp
from jax import lax
from jax.experimental import pallas as pl
from jax.experimental.pallas import tpu as pltpu
from jax.sharding import PartitionSpec as P

sharpness = 0.25
MESH = pl.DeviceIdType.MESH
BF = jnp.bfloat16
F32 = jnp.float32


def dot(x, y, dims):
    return lax.dot_general(x, y, (dims, ((), ())), preferred_element_type=F32)


def kernel(
    PB, PA, qh_hbm, ph_hbm, proj_hbm, clicks_hbm, bins_hbm,
    qg_ref, pg_ref, w_ref,
    clicks_ref, bins_ref, qraw, qh, ph, pht, proj, qe, pe, ebuf, pbuf, sc, gsend, grecv, tsend, trecv,
    wq, w1send, w1recv, w2send, w2recv,
    ls, qs, qr, ps, pr, ss, sr, gs, gr, ts, tr, us, ur, vs, vr,
):
    b = lax.axis_index("pb")
    a = lax.axis_index("pa")
    queries, token_local, hidden = qh_hbm.shape
    rows = queries * token_local
    E = proj.shape[1]
    tokens = PA * rows
    half = PB // 2
    parity = lax.rem(b, 2)
    level = b // 2

    def remote(src, dst, send, recv, to_b, to_a):
        return pltpu.make_async_remote_copy(
            src_ref=src, dst_ref=dst, send_sem=send, recv_sem=recv,
            device_id=(to_b, to_a), device_id_type=MESH,
        )

    loads = [
        pltpu.make_async_copy(qh_hbm, qraw, ls.at[0]),
        pltpu.make_async_copy(proj_hbm, proj, ls.at[1]),
        pltpu.make_async_copy(ph_hbm, ph, ls.at[2]),
        pltpu.make_async_copy(clicks_hbm, clicks_ref, ls.at[3]),
        pltpu.make_async_copy(bins_hbm, bins_ref, ls.at[4]),
    ]
    for c in loads:
        c.start()
    barrier = pltpu.get_barrier_semaphore()

    def greet(k, carry):
        other = lax.rem(b * PA + a + k, PB * PA)
        pl.semaphore_signal(
            barrier, inc=1, device_id=(other // PA, lax.rem(other, PA)), device_id_type=MESH
        )
        return carry

    lax.fori_loop(1, PB * PA, greet, 0)

    def group(k):
        return 2 * lax.rem(level + half - k // 2, half) + lax.rem(parity + k % 2, 2)

    def source(k):
        return 2 * lax.rem(level + k // 2, half) + lax.rem(parity + k % 2, 2)

    loads[0].wait()
    for q in range(queries):
        qh[q * token_local:(q + 1) * token_local] = qraw[q].astype(F32)
    loads[1].wait()
    qrows = qh[...].astype(BF)
    qe[a] = dot(qrows, proj[...], ((1,), (0,))).astype(BF)
    loads[2].wait()
    pe[b] = dot(ph[...], proj[...], ((1,), (0,))).astype(BF)
    pl.semaphore_wait(barrier, PB * PA - 1)

    query_in = []
    for o in range(1, PA):
        c = remote(qe.at[a], qe.at[a], qs.at[o - 1], qr.at[o - 1], b, lax.rem(a + o, PA))
        c.start()
        query_in.append(c)
    page_in = {}
    for k in range(PB - 1, 0, -1):
        c = remote(pe.at[b], pe.at[b], ps.at[k - 1], pr.at[k - 1], group(k), a)
        c.start()
        page_in[k] = c

    step = min(256, hidden)
    for s in range(0, hidden, step):
        pht[s:s + step] = ph[:, s:s + step].T

    for c in query_in:
        c.wait_recv()
    tok = qe[...].reshape(tokens, E)
    row = lax.broadcasted_iota(jnp.int32, (queries, tokens), 0) * token_local
    col = lax.broadcasted_iota(jnp.int32, (queries, tokens), 1)
    mask = jnp.zeros((queries, tokens), F32)
    for k in range(PA):
        low = row + k * rows
        mask = jnp.where((col >= low) & (col < low + token_local), 1.0, mask)
    maxes, sums = [], []
    for k in range(PB):
        if k:
            page_in[k].wait_recv()
        block = sharpness * dot(pe[source(k)], tok, ((1,), (1,)))
        top = jnp.max(block, axis=0, keepdims=True)
        e = jnp.exp(block - top)
        ebuf[k] = e
        maxes.append(top)
        sums.append(jnp.sum(e, axis=0, keepdims=True))
    top = functools.reduce(jnp.maximum, maxes)
    shrink = [jnp.exp(m - top) for m in maxes]
    total = functools.reduce(jnp.add, [s * f for s, f in zip(sums, shrink)])
    log_norm = top + jnp.log(total)
    score = jnp.sum(mask * log_norm, axis=1, keepdims=True)
    sc[a] = jnp.broadcast_to(score, sc.shape[1:])
    score_in = []
    for o in range(1, PA):
        c = remote(sc.at[a], sc.at[a], ss.at[o - 1], sr.at[o - 1], b, lax.rem(a + o, PA))
        c.start()
        score_in.append(c)

    unit = None
    for k in range(PB):
        soft = (ebuf[k] * (shrink[k] / total)).astype(BF)
        pbuf[k] = soft
        part = dot(soft, pe[source(k)], ((0,), (0,)))
        unit = part if unit is None else unit + part
    for k in range(PA):
        tsend[k] = unit[k * rows:(k + 1) * rows].astype(BF)
    token_in = []
    for o in range(1, PA):
        to = lax.rem(a + o, PA)
        c = remote(tsend.at[to], trecv.at[a], ts.at[o - 1], tr.at[o - 1], b, to)
        c.start()
        token_in.append(c)
    trecv[a] = tsend[a]

    loads[3].wait()
    loads[4].wait()
    pos = clicks_ref[:, 0, :]
    neg = clicks_ref[:, 1, :]
    pairs = pos.shape[1]
    weight = jnp.sqrt(bins_ref[...].astype(F32) + 1.0)
    for c in score_in:
        c.wait_recv()
    at_pos = jnp.zeros(pos.shape, F32)
    at_neg = jnp.zeros(pos.shape, F32)
    for p in range(PA):
        at_pos = at_pos + jnp.where(pos == p, sc[p][:, :pairs], 0.0)
        at_neg = at_neg + jnp.where(neg == p, sc[p][:, :pairs], 0.0)
    coeff = -weight * jax.nn.sigmoid(at_neg - at_pos)
    row = lax.broadcasted_iota(jnp.int32, (rows, queries), 0)
    col = lax.broadcasted_iota(jnp.int32, (rows, queries), 1) * token_local
    own = jnp.where((row >= col) & (row < col + token_local), 1.0, 0.0)

    def spread(page):
        hits = (pos == page).astype(F32) - (neg == page).astype(F32)
        grad = jnp.sum(coeff * hits, axis=1, keepdims=True)
        return sum(own[:, q:q + 1] * grad[q:q + 1] for q in range(queries))

    scaled = (qe[...].astype(F32) * spread(a)[None]).astype(BF).reshape(tokens, E)
    patch_in = []
    for k in range(PB - 1, -1, -1):
        patch_part = dot(pbuf[k], scaled, ((1,), (0,)))
        if k:
            gsend[k - 1] = patch_part.astype(BF)
            c = remote(
                gsend.at[k - 1], grecv.at[k - 1], gs.at[k - 1], gr.at[k - 1],
                source(k), a,
            )
            c.start()
            patch_in.append((k, c))
        else:
            patch_acc = patch_part

    for c in token_in:
        c.wait_recv()
    token_own = None
    for p in range(PA):
        part = trecv[p].astype(F32) * spread(p)
        token_own = part if token_own is None else token_own + part
    token_low = (sharpness * token_own).astype(BF)
    wq[...] = dot(qrows, token_low, ((0,), (0,)))
    qgrad = dot(token_low, proj[...], ((1,), (1,)))
    for q in range(queries):
        qg_ref[q] = qgrad[q * token_local:(q + 1) * token_local].astype(BF)

    for k, c in reversed(patch_in):
        c.wait_recv()
        patch_acc = patch_acc + grecv[k - 1].astype(F32)
    patch_low = (sharpness * patch_acc).astype(BF)

    partner = b + 1 - 2 * parity
    span = w1send.shape[1]
    chunk = w_ref.shape[0]
    def weight_block(index):
        base = pl.multiple_of(index * span, 8)
        return wq[pl.ds(base, span)] + dot(pht[pl.ds(base, span)], patch_low, ((1,), (0,)))

    pair_in = {}
    for m in range(half - 1, -1, -1):
        w1send[m] = weight_block(2 * lax.rem(level + m, half) + 1 - parity).astype(BF)
        c = remote(w1send.at[m], w1recv.at[m], us.at[m], ur.at[m], partner, a)
        c.start()
        pair_in[m] = c
    last_in = []
    weight_own = None
    for m in range(half - 1, -1, -1):
        to_level = lax.rem(level + m, half)
        mine = weight_block(2 * to_level + parity)
        pair_in[m].wait_recv()
        both = (mine + w1recv[m].astype(F32)).astype(BF)
        for k in range(PA):
            w2send[m * PA + k] = both[k * chunk:(k + 1) * chunk]
        for o in range(PA - 1, -1, -1):
            slot = m * PA + o
            if slot:
                to = lax.rem(a + o, PA)
                c = remote(
                    w2send.at[m * PA + to], w2recv.at[slot - 1], vs.at[slot - 1],
                    vr.at[slot - 1], 2 * to_level + parity, to,
                )
                c.start()
                last_in.append((slot, c))
    pg_ref[...] = dot(patch_low, proj[...], ((1,), (1,))).astype(BF)
    weight_sum = w2send[a].astype(F32)
    for slot, c in last_in:
        c.wait_recv()
        weight_sum = weight_sum + w2recv[slot - 1].astype(F32)
    w_ref[...] = weight_sum
    last_in = [c for _, c in last_in]
    pair_in = list(pair_in.values())
    for c in list(page_in.values()) + query_in + score_in + [c for _, c in patch_in] + token_in + pair_in + last_in:
        c.wait_send()


def writer(qg, pg, w, qg_out, pg_out, w_out, sems):
    copies = [
        pltpu.make_async_copy(pg, pg_out, sems.at[0]),
        pltpu.make_async_copy(qg, qg_out, sems.at[1]),
        pltpu.make_async_copy(w, w_out, sems.at[2]),
    ]
    for c in copies:
        c.start()
    for c in copies:
        c.wait()


def shards(PB, PA, query_hidden, page_hidden, projection, clicks, bins):
    queries, token_local, hidden = query_hidden.shape
    page_count, patches, _ = page_hidden.shape
    assert page_count == 1 and PB % 2 == 0
    E = projection.shape[1]
    rows = queries * token_local
    tokens = rows * PA
    chunk = hidden // (PB * PA)
    half = PB // 2
    count = half * PA
    ph = page_hidden.reshape(patches, hidden)
    vmem = pl.BlockSpec(memory_space=pltpu.VMEM)
    hbm = pl.BlockSpec(memory_space=pltpu.HBM)
    dma = lambda n: pltpu.SemaphoreType.DMA((n,))
    outs = (
        jax.ShapeDtypeStruct(query_hidden.shape, BF),
        jax.ShapeDtypeStruct((patches, hidden), BF),
        jax.ShapeDtypeStruct((chunk, E), F32),
    )
    results = pl.pallas_call(
        functools.partial(kernel, PB, PA),
        out_shape=tuple(pltpu.VMEM(o.shape, o.dtype) for o in outs),
        in_specs=[hbm] * 5,
        out_specs=(vmem,) * 3,
        scratch_shapes=[
            pltpu.VMEM((queries, 2, clicks.shape[1]), jnp.int32),
            pltpu.VMEM(bins.shape, jnp.int32),
            pltpu.VMEM(query_hidden.shape, BF),
            pltpu.VMEM((rows, hidden), F32),
            pltpu.VMEM((patches, hidden), BF),
            pltpu.VMEM((hidden, patches), BF),
            pltpu.VMEM((hidden, E), BF),
            pltpu.VMEM((PA, rows, E), BF),
            pltpu.VMEM((PB, patches, E), BF),
            pltpu.VMEM((PB, patches, tokens), F32),
            pltpu.VMEM((PB, patches, tokens), BF),
            pltpu.VMEM((PA, queries, 128), F32),
            pltpu.VMEM((PB - 1, patches, E), BF),
            pltpu.VMEM((PB - 1, patches, E), BF),
            pltpu.VMEM((PA, rows, E), BF),
            pltpu.VMEM((PA, rows, E), BF),
            pltpu.VMEM((hidden, E), F32),
            pltpu.VMEM((half, PA * chunk, E), BF),
            pltpu.VMEM((half, PA * chunk, E), BF),
            pltpu.VMEM((count, chunk, E), BF),
            pltpu.VMEM((count - 1, chunk, E), BF),
            dma(5), dma(PA - 1), dma(PA - 1), dma(PB - 1), dma(PB - 1), dma(PA - 1), dma(PA - 1),
            dma(PB - 1), dma(PB - 1), dma(PA - 1), dma(PA - 1), dma(half), dma(half),
            dma(count - 1), dma(count - 1),
        ],
        compiler_params=pltpu.CompilerParams(
            collective_id=0, has_side_effects=True, vmem_limit_bytes=65536000
        ),
        name="fused",
    )(query_hidden, ph, projection, jnp.transpose(clicks, (0, 2, 1)), bins)
    query_grad, page_grad, weight_grad = pl.pallas_call(
        writer,
        out_shape=outs,
        in_specs=[vmem] * 3,
        out_specs=(hbm,) * 3,
        scratch_shapes=[dma(3)],
        compiler_params=pltpu.CompilerParams(vmem_limit_bytes=4 * 1024 * 1024),
        name="writer",
    )(*results)
    return query_grad, page_grad.reshape(page_hidden.shape), weight_grad


def solution(mesh):
    return jax.shard_map(
        functools.partial(shards, mesh.shape["pb"], mesh.shape["pa"]),
        mesh=mesh,
        in_specs=(
            P("pb", "pa", None),
            P("pa", "pb", None),
            P(),
            P("pb", None, None),
            P("pb", None),
        ),
        out_specs=(P("pb", "pa", None), P("pa", "pb", None), P(("pb", "pa"), None)),
        check_vma=False,
    )
```

time: 39.6 us -> 33.5 us (0.85)
  the two profiles are of different devices: /device:TPU:1 before, /device:TPU:0 now
where the time goes in v2:
time: 33.5 us; the launch traced here: 33.3 us
  Pallas kernels  32.7 us (98%)
  between operations  0.64 us (2%)
    pallas_call x1, Pallas kernels, shards(): pl.pallas_call(functools.partial(kernel, PB, PA), out_shape=tuple((pltpu....  31.6 us
    pallas_call x1, Pallas kernels, shards(): pl.pallas_call(writer, out_shape=outs, in_specs=[vmem] * 3, out_specs=(hb...  1.03 us

profile of v2, /device:TPU:0, one launch (start us, length us, event | category | flops | bytes accessed | tf_op | source)
XLA Modules:
  0.0 33.3 jit_solution(675301423675010217)
XLA Ops:
  0.6 31.6 %fused.1 = (bf16[8,4,2048]{2,1,0:T(4,128)(2,1)S(1)}, bf16[256,2048]{1,0:T(8,128)(2,1)S(1)}, f32[64,128]{1,0:T(8,128)S(1)}) custom-call(bf16[8,4,2048]{2,1,0:T(4,128)(2,1)} %qh_hbm.1, bf16[256,2048]{1,0:T(8,128)(2,1)} %bitcast.3, bf16[2048,128]{1,0:T(8,128)(2,1)} %proj_hbm.1, s32[8,2,8]{2,1,0:T(2,128)} %bitcast.4, s32[8,8]{1,0:T(8,128)} %bins_hbm.1), custom_call_target="tpu_custom_call" | custom-call | tf_op jit(solution)/shard_map/fused/pallas_call | solution.py:271
  32.3 1.0 %writer.1 = (bf16[8,4,2048]{2,1,0:T(4,128)(2,1)}, bf16[256,2048]{1,0:T(8,128)(2,1)}, f32[64,128]{1,0:T(8,128)}) custom-call(bf16[8,4,2048]{2,1,0:T(4,128)(2,1)S(1)} %get-tuple-element.9.qg, bf16[256,2048]{1,0:T(8,128)(2,1)S(1)} %get-tuple-element.10.pg, f32[64,128]{1,0:T(8,128)S(1)} %get-tuple-element.11.w), custom_call_target="tpu_custom_call" | custom-call | tf_op jit(solution)/shard_map/writer/pallas_call | solution.py:307

commit v3 on v2

--- a/solution.py
+++ b/solution.py
@@ -51,14 +51,14 @@
         c.start()
     barrier = pltpu.get_barrier_semaphore()
 
-    def greet(k, carry):
-        other = lax.rem(b * PA + a + k, PB * PA)
+    for o in range(1, PA):
         pl.semaphore_signal(
-            barrier, inc=1, device_id=(other // PA, lax.rem(other, PA)), device_id_type=MESH
+            barrier, inc=1, device_id=(b, lax.rem(a + o, PA)), device_id_type=MESH
         )
-        return carry
-
-    lax.fori_loop(1, PB * PA, greet, 0)
+    for o in range(1, PB):
+        pl.semaphore_signal(
+            barrier, inc=1, device_id=(lax.rem(b + o, PB), a), device_id_type=MESH
+        )
 
     def group(k):
         return 2 * lax.rem(level + half - k // 2, half) + lax.rem(parity + k % 2, 2)
@@ -74,7 +74,7 @@
     qe[a] = dot(qrows, proj[...], ((1,), (0,))).astype(BF)
     loads[2].wait()
     pe[b] = dot(ph[...], proj[...], ((1,), (0,))).astype(BF)
-    pl.semaphore_wait(barrier, PB * PA - 1)
+    pl.semaphore_wait(barrier, PB + PA - 2)
 
     query_in = []
     for o in range(1, PA):

time: 33.5 us -> 32 us (0.955)
  Pallas kernels: 32.7 us -> 31.2 us
    pallas_call x1, Pallas kernels: 31.6 us -> 30.2 us  [shards(): pl.pallas_call(functools.partial(kernel, PB, PA), out_shape=tuple((pltpu....]
where the time goes in v3:
time: 32 us; the launch traced here: 31.9 us
  Pallas kernels  31.2 us (98%)
  between operations  0.64 us (2%)
    pallas_call x1, Pallas kernels, shards(): pl.pallas_call(functools.partial(kernel, PB, PA), out_shape=tuple((pltpu....  30.2 us
    pallas_call x1, Pallas kernels, shards(): pl.pallas_call(writer, out_shape=outs, in_specs=[vmem] * 3, out_specs=(hb...  1.03 us

profile of v3, /device:TPU:0, one launch (start us, length us, event | category | flops | bytes accessed | tf_op | source)
XLA Modules:
  0.0 31.9 jit_solution(6915643921635424744)
XLA Ops:
  0.6 30.2 %fused.1 = (bf16[8,4,2048]{2,1,0:T(4,128)(2,1)S(1)}, bf16[256,2048]{1,0:T(8,128)(2,1)S(1)}, f32[64,128]{1,0:T(8,128)S(1)}) custom-call(bf16[8,4,2048]{2,1,0:T(4,128)(2,1)} %qh_hbm.1, bf16[256,2048]{1,0:T(8,128)(2,1)} %bitcast.3, bf16[2048,128]{1,0:T(8,128)(2,1)} %proj_hbm.1, s32[8,2,8]{2,1,0:T(2,128)} %bitcast.4, s32[8,8]{1,0:T(8,128)} %bins_hbm.1), custom_call_target="tpu_custom_call" | custom-call | tf_op jit(solution)/shard_map/fused/pallas_call | solution.py:271
  30.9 1.0 %writer.1 = (bf16[8,4,2048]{2,1,0:T(4,128)(2,1)}, bf16[256,2048]{1,0:T(8,128)(2,1)}, f32[64,128]{1,0:T(8,128)}) custom-call(bf16[8,4,2048]{2,1,0:T(4,128)(2,1)S(1)} %get-tuple-element.9.qg, bf16[256,2048]{1,0:T(8,128)(2,1)S(1)} %get-tuple-element.10.pg, f32[64,128]{1,0:T(8,128)S(1)} %get-tuple-element.11.w), custom_call_target="tpu_custom_call" | custom-call | tf_op jit(solution)/shard_map/writer/pallas_call | solution.py:307
